TPU v7x, 32 devices: a whole 2x2x4 slice. The times are simulated.
32 devices in a mesh: grp: 4 (over y, x), dev: 8 (over z, core).
Axes of the slice: x: 2, y: 2, z: 4, core: 2. Of those that a mesh axis runs over, the one named last changes fastest.
Arguments:
- nz_user: int32 [4096, 128], P(('grp', 'dev')), may hold values from 0 to 8191
- nz_sub: int32 [4096, 128], P(('grp', 'dev')), may hold values from 0 to 2047
- nz_value: float32 [4096, 128], P(('grp', 'dev')), may hold values from -1 to 1
- tile_word: int32 [4096], P(('grp', 'dev')), may hold values from 0 to 2047, as said below
- word_owner: int32 [2048], replicated, may hold values from 0 to 2047, as said below
- user_factor: bfloat16 [64, 8192], P(None, 'dev'), may hold values from -6 to 6
- sub_factor: bfloat16 [64, 2048], P(None, 'dev'), may hold values from -6 to 6
Outputs:
- word_rows: float32 [64, 2048], P(None, ('grp', 'dev'))
Inputs may be any that keep to these rules, and one draw needn't show every extreme that they name: A permutation of the word indices: word w is summed into column word_owner[w] of word_rows. `tile_word`: tile i lies on device i // 128 (grp+dev order). On every device at most 2 tiles belong to words whose output column lies on any one other device, and on every device that bound is reached for some other device.
All inputs are finite; a program needn't handle non-finite values.
Results may differ from a plain program's by a relative error of at most 0.0003.
Values may be sent and summed in bfloat16 or wider, within the bound.
A program may use at most 64 MiB of HBM per device.

v0:
```python
import jax
import jax.numpy as jnp
from jax import lax
from jax.sharding import PartitionSpec as P

CAP = 2


def tile_sums(user_table, sub_table, nz_user, nz_sub, nz_value):
    tile_count, tile_width = nz_user.shape
    block_tiles = min(tile_count, 128)
    block_count = tile_count // block_tiles

    def one_block(block_args):
        users_block, subs_block, vals_block = block_args
        user_rows = jnp.take(user_table, users_block, axis=0).astype(jnp.float32)
        sub_rows = jnp.take(sub_table, subs_block, axis=0).astype(jnp.float32)
        return jnp.sum(user_rows * sub_rows * vals_block[:, :, None], axis=1)

    block_sums = lax.map(
        one_block,
        (
            nz_user.reshape(block_count, block_tiles, tile_width),
            nz_sub.reshape(block_count, block_tiles, tile_width),
            nz_value.reshape(block_count, block_tiles, tile_width),
        ),
    )
    return block_sums.reshape(tile_count, block_sums.shape[2])


def shards(nz_user, nz_sub, nz_value, tile_word, word_owner, user_factor, sub_factor):
    users_all, subs_all = (
        lax.all_gather(user_factor, "dev", axis=1, tiled=True),
        lax.all_gather(sub_factor, "dev", axis=1, tiled=True),
    )
    user_table = jnp.transpose(users_all)
    sub_table = jnp.transpose(subs_all)
    tile_rows = tile_sums(user_table, sub_table, nz_user, nz_sub, nz_value)
    tile_count, rank_width = tile_rows.shape
    grp_size = lax.axis_size("grp")
    dev_size = lax.axis_size("dev")
    devices_all = grp_size * dev_size
    words_total = word_owner.shape[0]
    words_local = words_total // devices_all
    out_rows = jnp.take(word_owner, tile_word)
    self_index = lax.axis_index("grp") * dev_size + lax.axis_index("dev")
    owner_dev = out_rows // words_local
    local_row = out_rows - owner_dev * words_local
    owned = owner_dev == self_index
    columns = jnp.arange(words_local, dtype=jnp.int32)
    own_table = (owned[:, None] & (local_row[:, None] == columns[None, :])).astype(jnp.float32)
    own_part = jnp.einsum("tr,tk->rk", tile_rows, own_table, precision=lax.Precision.HIGHEST)
    peer_ids = jnp.arange(devices_all, dtype=jnp.int32)
    outgoing = (jnp.logical_not(owned)[:, None] & (owner_dev[:, None] == peer_ids[None, :])).astype(
        jnp.float32
    )
    tile_ids = jnp.arange(tile_count, dtype=jnp.int32)
    earlier_table = (tile_ids[:, None] > tile_ids[None, :]).astype(jnp.float32)
    earlier = jnp.dot(
        earlier_table, outgoing, precision=lax.Precision.HIGHEST, preferred_element_type=jnp.float32
    )
    position = jnp.sum(earlier * outgoing, axis=1).astype(jnp.int32)
    send_slot = jnp.where(owned, devices_all * CAP, owner_dev * CAP + position)
    slot_ids = jnp.arange(devices_all * CAP, dtype=jnp.int32)
    slot_table = (send_slot[:, None] == slot_ids[None, :]).astype(jnp.float32)
    send_rows = jnp.einsum("ts,tr->sr", slot_table, tile_rows, precision=lax.Precision.HIGHEST)
    filled = jnp.sum(slot_table, axis=0)
    send_ids = (
        jnp.dot(
            local_row.astype(jnp.float32),
            slot_table,
            precision=lax.Precision.HIGHEST,
            preferred_element_type=jnp.float32,
        )
        + filled
        - 1.0
    )
    send_rows = send_rows.reshape(grp_size, dev_size, CAP * rank_width)
    send_ids = send_ids.reshape(grp_size, dev_size, CAP)
    got_rows, got_ids = (
        lax.all_to_all(
            lax.all_to_all(send_rows, "grp", split_axis=0, concat_axis=0, tiled=True),
            "dev",
            split_axis=1,
            concat_axis=1,
            tiled=True,
        ),
        lax.all_to_all(
            lax.all_to_all(send_ids, "grp", split_axis=0, concat_axis=0, tiled=True),
            "dev",
            split_axis=1,
            concat_axis=1,
            tiled=True,
        ),
    )
    got_rows = got_rows.reshape(devices_all * CAP, rank_width)
    got_ids = got_ids.reshape(devices_all * CAP).astype(jnp.int32)
    got_table = (got_ids[:, None] == columns[None, :]).astype(jnp.float32)
    far_part = jnp.einsum("sr,sk->rk", got_rows, got_table, precision=lax.Precision.HIGHEST)
    return own_part + far_part


def solution(mesh):
    return jax.shard_map(
        shards,
        mesh=mesh,
        in_specs=(
            P(("grp", "dev"), None),
            P(("grp", "dev"), None),
            P(("grp", "dev"), None),
            P(("grp", "dev")),
            P(),
            P(None, "dev"),
            P(None, "dev"),
        ),
        out_specs=P(None, ("grp", "dev")),
        check_vma=False,
    )
```

profile of v0, /device:TPU:0, one launch (start us, length us, event | category | flops | bytes accessed | tf_op | source)
XLA Modules:
  0.0 198.2 jit_solution(13226460569784429638)
XLA Ops:
  6.5 1.8 copy.39
  8.3 0.7 compare_select_fusion.2
  9.0 1.1 gather_fusion.2
  10.2 0.7 fusion.16
  10.8 0.2 fusion
  11.0 0.7 add_select_fusion
  11.7 0.1 convert_reduce_fusion
  11.8 0.1 fusion.2
  11.9 0.1 reshape.81
  12.1 0.7 copy.43
  12.7 5.2 %all-to-all-start.2 = ((f32[4,8,2]{1,2,0:T(2,128)}), f32[4,8,2]{1,2,0:T(2,128)S(1)}, u32[]{:S(2)}, u32[]{:S(2)}) async-start(f32[4,8,2]{1,2,0:T(2,128)} %copy.43), calls=%async_computation.2 | async-start | bytes 8192 | tf_op jit(solution)/shard_map/all_to_all | solution.py:89
  17.9 0.9 copy.40
  18.8 0.9 compare_and_fusion
  19.7 0.9 bitcast_clamp_fusion.1
  20.6 0.9 bitcast_clamp_fusion
  21.5 17.7 %all_gather.7 = bf16[64,2048]{0,1:T(8,128)(2,1)S(1)} all-gather(bf16[64,256]{0,1:T(8,128)(2,1)S(1)} %copy.40), channel_id=1, replica_groups=mesh['grp'=4,'dev'=8] {'dev'}, dimensions={1}, use_global_device_ids=true | all-gather | bytes 294912 | tf_op jit(solution)/shard_map/all_gather | solution.py:34
  39.1 57.4 %gather_fusion.1 = bf16[16384,64]{1,0:T(8,128)(2,1)} fusion(bf16[2048,64]{1,0:T(8,128)(2,1)S(1)} %bitcast.22, s32[16384]{0:T(1024)S(1)} %bitcast_clamp_fusion), kind=kCustom, calls=%fused_computation.1 | custom fusion | bytes 4259840 | tf_op jit(solution)/shard_map/while/body/eval_jaxpr/jit(_take)/gather | solution.py:17
  96.5 0.7 copy.44
  97.2 4.8 %all-to-all-start.3 = ((f32[4,8,2]{0,2,1:T(2,128)}), f32[4,8,2]{0,2,1:T(2,128)S(1)}, u32[]{:S(2)}, u32[]{:S(2)}) async-start(f32[4,8,2]{0,2,1:T(2,128)} %copy.44), calls=%async_computation.3 | async-start | bytes 16384 | tf_op jit(solution)/shard_map/all_to_all | solution.py:88
  102.0 56.8 %gather_fusion = bf16[16384,64]{1,0:T(8,128)(2,1)} fusion(bf16[8192,64]{1,0:T(8,128)(2,1)} %bitcast.23, s32[16384]{0:T(1024)S(1)} %bitcast_clamp_fusion.1), kind=kCustom, calls=%fused_computation | custom fusion | bytes 4259840 | tf_op jit(solution)/shard_map/while/body/eval_jaxpr/jit(_take)/gather | solution.py:16
  158.8 10.6 %multiply_reduce_fusion = f32[128,64]{1,0:T(8,128)S(1)} fusion(f32[128,128]{1,0:T(8,128)S(1)} %copy-done.1, pred[128,128]{1,0:T(8,128)(4,1)S(1)} %get-tuple-element.30, pred[128,128]{1,0:T(8,128)(4,1)S(1)} %get-tuple-element.32, bf16[16384,64]{1,0:T(8,128)(2,1)} %gather_fusion.1, bf16[16384,64]{1,0:T(8,128)(2,1)} %gather_fusion), kind=kLoop, calls=%fused_computation.3 | loop fusion | flops 7331840 | bytes 4325376 | tf_op jit(solution)/shard_map/while/body/eval_jaxpr/reduce_sum | solution.py:18
  169.4 0.2 fusion.6
  169.6 0.7 reshape.79
  170.3 4.1 %all-to-all-start = ((f32[4,8,128]{2,1,0:T(8,128)}), f32[4,8,128]{2,1,0:T(8,128)S(1)}, u32[]{:S(2)}, u32[]{:S(2)}) async-start(f32[4,8,128]{2,1,0:T(8,128)} %reshape.79), calls=%async_computation | async-start | bytes 32768 | tf_op jit(solution)/shard_map/all_to_all | solution.py:82
  174.5 0.1 copy.46
  174.6 0.1 convert_element_type.39
  174.7 4.4 %all-to-all-done = f32[4,8,128]{2,1,0:T(8,128)S(1)} async-done(((f32[4,8,128]{2,1,0:T(8,128)}), f32[4,8,128]{2,1,0:T(8,128)S(1)}, u32[]{:S(2)}, u32[]{:S(2)}) %all-to-all-start) | async-done | bytes 16416 | tf_op jit(solution)/shard_map/all_to_all | solution.py:82
  179.1 0.6 copy.41
  179.7 5.1 %all-to-all-start.1 = ((f32[4,8,128]{2,0,1:T(4,128)}), f32[4,8,128]{2,0,1:T(4,128)S(1)}, u32[]{:S(2)}, u32[]{:S(2)}) async-start(f32[4,8,128]{2,0,1:T(4,128)} %copy.41), calls=%async_computation.1 | async-start | bytes 32768 | tf_op jit(solution)/shard_map/all_to_all | solution.py:81
  184.8 0.3 fusion.4
  185.1 5.4 %all-to-all-done.1 = f32[4,8,128]{2,0,1:T(4,128)S(1)} async-done(((f32[4,8,128]{2,0,1:T(4,128)}), f32[4,8,128]{2,0,1:T(4,128)S(1)}, u32[]{:S(2)}, u32[]{:S(2)}) %all-to-all-start.1) | async-done | bytes 16416 | tf_op jit(solution)/shard_map/all_to_all | solution.py:81
  190.5 0.9 convolution_add_fusion
  (14 shorter events, 0.2 us)
Async XLA Ops:
  6.5 2.5 %copy-start = (s32[2048]{0:T(1024)S(1)}, s32[2048]{0:T(1024)}, u32[]{:S(2)}) copy-start(s32[2048]{0:T(1024)} %param.11) | copy-start | bytes 24580
  6.5 95.5 %all-gather.2.cloned.1.call-start = ((), (), s32[]{:S(2)}) async-start(), calls=%async_computation.4 | async-start | bytes 2359296 | tf_op jit(solution)/shard_map/all_gather | solution.py:33
  12.7 83.8 %all-to-all-start.2 = ((f32[4,8,2]{1,2,0:T(2,128)}), f32[4,8,2]{1,2,0:T(2,128)S(1)}, u32[]{:S(2)}, u32[]{:S(2)}) async-start(f32[4,8,2]{1,2,0:T(2,128)} %copy.43), calls=%async_computation.2 | async-start | bytes 8192 | tf_op jit(solution)/shard_map/all_to_all | solution.py:89
  97.2 73.1 %all-to-all-start.3 = ((f32[4,8,2]{0,2,1:T(2,128)}), f32[4,8,2]{0,2,1:T(2,128)S(1)}, u32[]{:S(2)}, u32[]{:S(2)}) async-start(f32[4,8,2]{0,2,1:T(2,128)} %copy.44), calls=%async_computation.3 | async-start | bytes 16384 | tf_op jit(solution)/shard_map/all_to_all | solution.py:88
  102.0 56.8 %copy-start.1 = (f32[128,128]{1,0:T(8,128)S(1)}, f32[128,128]{1,0:T(8,128)}, u32[]{:S(2)}) copy-start(f32[128,128]{1,0:T(8,128)} %param.9) | copy-start | bytes 196612
  170.3 8.8 %all-to-all-start = ((f32[4,8,128]{2,1,0:T(8,128)}), f32[4,8,128]{2,1,0:T(8,128)S(1)}, u32[]{:S(2)}, u32[]{:S(2)}) async-start(f32[4,8,128]{2,1,0:T(8,128)} %reshape.79), calls=%async_computation | async-start | bytes 32768 | tf_op jit(solution)/shard_map/all_to_all | solution.py:82
  179.7 10.7 %all-to-all-start.1 = ((f32[4,8,128]{2,0,1:T(4,128)}), f32[4,8,128]{2,0,1:T(4,128)S(1)}, u32[]{:S(2)}, u32[]{:S(2)}) async-start(f32[4,8,128]{2,0,1:T(4,128)} %copy.41), calls=%async_computation.1 | async-start | bytes 32768 | tf_op jit(solution)/shard_map/all_to_all | solution.py:81
Sparse Core Ops, SparseCore 0:
  8.9 36.0 all-gather.1
where the time goes:
time: 199 us; the launch traced here: 198 us
  local copies, waits for them, and re-layouts  121 us (61%)
  starting transfers between devices  19.2 us (10%)
  blocking collectives  17.7 us (9%)
  other arithmetic  15.4 us (8%)
  between operations  13.5 us (7%)
  waiting for transfers between devices  9.81 us (5%)
    gather x1, local copies, waits for them, and re-layouts, one_block(): sub_rows = jnp.take(sub_table, subs_block, axis=0).astype(jnp.float32)  57.4 us
    gather x1, local copies, waits for them, and re-layouts, one_block(): user_rows = jnp.take(user_table, users_block, axis=0).astype(jnp.float32)  56.8 us
    all_gather x1, blocking collectives, shards(): lax.all_gather(sub_factor, 'dev', axis=1, tiled=True)  17.7 us
    reduce_sum x1, other arithmetic, one_block(): return jnp.sum(user_rows * sub_rows * vals_block[:, :, None], axis=1)  10.6 us
    all_to_all x1, waiting for transfers between devices, shards(): lax.all_to_all(lax.all_to_all(send_rows, 'grp', split_axis=0, concat_axis...  5.38 us
    all_to_all x1, starting transfers between devices, shards(): lax.all_to_all(send_ids, 'grp', split_axis=0, concat_axis=0, tiled=True)  5.19 us
    all_to_all x1, starting transfers between devices, shards(): lax.all_to_all(lax.all_to_all(send_rows, 'grp', split_axis=0, concat_axis...  5.08 us
    all_to_all x1, starting transfers between devices, shards(): lax.all_to_all(lax.all_to_all(send_ids, 'grp', split_axis=0, concat_axis=...  4.77 us
  transfers between devices with their start and end apart: 5, of which 2 were waited for; matrix products, arithmetic and copies ran while one was open for 68% of the time, Pallas kernels for 0%

commit v1 on v0

--- a/solution.py
+++ b/solution.py
@@ -85,12 +85,20 @@
             concat_axis=1,
             tiled=True,
         ),
-        lax.all_to_all(
-            lax.all_to_all(send_ids, "grp", split_axis=0, concat_axis=0, tiled=True),
-            "dev",
-            split_axis=1,
-            concat_axis=1,
-            tiled=True,
+        jnp.concatenate(
+            lax.all_to_all(
+                jnp.stack(
+                    jnp.split(
+                        lax.all_to_all(send_ids, "grp", split_axis=0, concat_axis=0, tiled=True),
+                        lax.axis_size("dev"),
+                        axis=1,
+                    )
+                ),
+                "dev",
+                0,
+                0,
+            ),
+            axis=1,
         ),
     )
     got_rows = got_rows.reshape(devices_all * CAP, rank_width)

time: 199 us -> 204 us (1.025)
  local copies, waits for them, and re-layouts: 121 us -> 127 us
    unnamed x6 -> x13, local copies, waits for them, and re-layouts: 2.64 us -> 6.49 us
where the time goes in v1:
time: 204 us; the launch traced here: 203 us
  local copies, waits for them, and re-layouts  127 us (62%)
  starting transfers between devices  19.3 us (9%)
  blocking collectives  16.7 us (8%)
  other arithmetic  15.4 us (8%)
  between operations  13.5 us (7%)
  waiting for transfers between devices  9.87 us (5%)
    gather x1, local copies, waits for them, and re-layouts, one_block(): sub_rows = jnp.take(sub_table, subs_block, axis=0).astype(jnp.float32)  57.8 us
    gather x1, local copies, waits for them, and re-layouts, one_block(): user_rows = jnp.take(user_table, users_block, axis=0).astype(jnp.float32)  57.3 us
    all_gather x1, blocking collectives, shards(): lax.all_gather(sub_factor, 'dev', axis=1, tiled=True)  16.7 us
    reduce_sum x1, other arithmetic, one_block(): return jnp.sum(user_rows * sub_rows * vals_block[:, :, None], axis=1)  10.6 us
    unnamed x13, local copies, waits for them, and re-layouts  6.49 us
    all_to_all x1, waiting for transfers between devices, shards(): lax.all_to_all(lax.all_to_all(send_rows, 'grp', split_axis=0, concat_axis...  5.38 us
    all_to_all x1, starting transfers between devices, shards(): lax.all_to_all(send_ids, 'grp', split_axis=0, concat_axis=0, tiled=True)  5.19 us
    all_to_all x1, starting transfers between devices, shards(): lax.all_to_all(lax.all_to_all(send_rows, 'grp', split_axis=0, concat_axis...  5.07 us
  transfers between devices with their start and end apart: 5, of which 2 were waited for; matrix products, arithmetic and copies ran while one was open for 68% of the time, Pallas kernels for 0%

profile of v1, /device:TPU:0, one launch (start us, length us, event | category | flops | bytes accessed | tf_op | source)
XLA Modules:
  0.0 203.0 jit_solution(2702232803094259269)
XLA Ops:
  6.5 0.7 compare_select_fusion.2
  7.2 1.1 gather_fusion.2
  8.4 0.7 fusion.16
  9.2 0.7 add_select_fusion
  10.3 0.7 copy.75
  11.0 5.2 %all-to-all-start.2 = ((f32[4,8,2]{1,2,0:T(2,128)}), f32[4,8,2]{1,2,0:T(2,128)S(1)}, u32[]{:S(2)}, u32[]{:S(2)}) async-start(f32[4,8,2]{1,2,0:T(2,128)} %copy.75), calls=%async_computation.2 | async-start | bytes 8192 | tf_op jit(solution)/shard_map/all_to_all | solution.py:92
  16.2 1.7 copy.71
  17.9 0.9 bitcast_clamp_fusion.1
  18.8 0.9 compare_and_fusion
  19.7 0.9 bitcast_clamp_fusion
  20.6 0.9 copy.72
  21.5 16.7 %all_gather.7 = bf16[64,2048]{0,1:T(8,128)(2,1)S(1)} all-gather(bf16[64,256]{0,1:T(8,128)(2,1)S(1)} %copy.72), channel_id=1, replica_groups=mesh['grp'=4,'dev'=8] {'dev'}, dimensions={1}, use_global_device_ids=true | all-gather | bytes 294912 | tf_op jit(solution)/shard_map/all_gather | solution.py:34
  38.2 57.8 %gather_fusion.1 = bf16[16384,64]{1,0:T(8,128)(2,1)} fusion(bf16[2048,64]{1,0:T(8,128)(2,1)S(1)} %bitcast.44, s32[16384]{0:T(1024)S(1)} %bitcast_clamp_fusion), kind=kCustom, calls=%fused_computation.1 | custom fusion | bytes 4259840 | tf_op jit(solution)/shard_map/while/body/eval_jaxpr/jit(_take)/gather | solution.py:17
  96.9 0.5 constant_dynamic-update-slice_fusion.7
  97.4 0.5 constant_dynamic-update-slice_fusion.6
  97.9 0.6 constant_dynamic-update-slice_fusion.5
  98.5 0.6 constant_dynamic-update-slice_fusion.4
  99.1 0.5 constant_dynamic-update-slice_fusion.3
  99.6 0.5 constant_dynamic-update-slice_fusion.2
  100.1 0.6 constant_dynamic-update-slice_fusion.1
  100.7 0.6 constant_dynamic-update-slice_fusion
  101.3 4.9 %all-to-all-start.3 = ((f32[8,4,1,2]{1,3,2,0:T(2,128)}), f32[8,4,1,2]{1,3,2,0:T(2,128)S(1)}, u32[]{:S(2)}, u32[]{:S(2)}) async-start(f32[8,4,1,2]{1,3,2,0:T(2,128)} %constant_dynamic-update-slice_fusion), calls=%async_computation.3 | async-start | bytes 16384 | tf_op jit(solution)/shard_map/all_to_all | solution.py:89
  106.3 57.3 %gather_fusion = bf16[16384,64]{1,0:T(8,128)(2,1)} fusion(bf16[8192,64]{1,0:T(8,128)(2,1)} %bitcast.45, s32[16384]{0:T(1024)S(1)} %bitcast_clamp_fusion.1), kind=kCustom, calls=%fused_computation | custom fusion | bytes 4259840 | tf_op jit(solution)/shard_map/while/body/eval_jaxpr/jit(_take)/gather | solution.py:16
  163.6 10.6 %multiply_reduce_fusion = f32[128,64]{1,0:T(8,128)S(1)} fusion(f32[128,128]{1,0:T(8,128)S(1)} %copy-done.1, pred[128,128]{1,0:T(8,128)(4,1)S(1)} %get-tuple-element.39, pred[128,128]{1,0:T(8,128)(4,1)S(1)} %get-tuple-element.40, bf16[16384,64]{1,0:T(8,128)(2,1)} %gather_fusion.1, bf16[16384,64]{1,0:T(8,128)(2,1)} %gather_fusion), kind=kLoop, calls=%fused_computation.3 | loop fusion | flops 7331840 | bytes 4325376 | tf_op jit(solution)/shard_map/while/body/eval_jaxpr/reduce_sum | solution.py:18
  174.3 0.7 reshape.79
  175.0 4.1 %all-to-all-start = ((f32[4,8,128]{2,1,0:T(8,128)}), f32[4,8,128]{2,1,0:T(8,128)S(1)}, u32[]{:S(2)}, u32[]{:S(2)}) async-start(f32[4,8,128]{2,1,0:T(8,128)} %reshape.79), calls=%async_computation | async-start | bytes 32768 | tf_op jit(solution)/shard_map/all_to_all | solution.py:82
  179.4 4.5 %all-to-all-done = f32[4,8,128]{2,1,0:T(8,128)S(1)} async-done(((f32[4,8,128]{2,1,0:T(8,128)}), f32[4,8,128]{2,1,0:T(8,128)S(1)}, u32[]{:S(2)}, u32[]{:S(2)}) %all-to-all-start) | async-done | bytes 16416 | tf_op jit(solution)/shard_map/all_to_all | solution.py:82
  183.9 0.6 copy.73
  184.5 5.1 %all-to-all-start.1 = ((f32[4,8,128]{2,0,1:T(4,128)}), f32[4,8,128]{2,0,1:T(4,128)S(1)}, u32[]{:S(2)}, u32[]{:S(2)}) async-start(f32[4,8,128]{2,0,1:T(4,128)} %copy.73), calls=%async_computation.1 | async-start | bytes 32768 | tf_op jit(solution)/shard_map/all_to_all | solution.py:81
  189.5 0.3 fusion.4
  189.8 5.4 %all-to-all-done.1 = f32[4,8,128]{2,0,1:T(4,128)S(1)} async-done(((f32[4,8,128]{2,0,1:T(4,128)}), f32[4,8,128]{2,0,1:T(4,128)S(1)}, u32[]{:S(2)}, u32[]{:S(2)}) %all-to-all-start.1) | async-done | bytes 16416 | tf_op jit(solution)/shard_map/all_to_all | solution.py:81
  195.3 0.9 convolution_add_fusion
  (29 shorter events, 2.0 us)
Async XLA Ops:
  6.5 0.7 copy-start
  11.0 85.0 %all-to-all-start.2 = ((f32[4,8,2]{1,2,0:T(2,128)}), f32[4,8,2]{1,2,0:T(2,128)S(1)}, u32[]{:S(2)}, u32[]{:S(2)}) async-start(f32[4,8,2]{1,2,0:T(2,128)} %copy.75), calls=%async_computation.2 | async-start | bytes 8192 | tf_op jit(solution)/shard_map/all_to_all | solution.py:92
  16.2 90.1 %all-gather.2.cloned.1.call-start = ((), (), s32[]{:S(2)}) async-start(), calls=%async_computation.4 | async-start | bytes 2359296 | tf_op jit(solution)/shard_map/all_gather | solution.py:33
  101.3 73.7 %all-to-all-start.3 = ((f32[8,4,1,2]{1,3,2,0:T(2,128)}), f32[8,4,1,2]{1,3,2,0:T(2,128)S(1)}, u32[]{:S(2)}, u32[]{:S(2)}) async-start(f32[8,4,1,2]{1,3,2,0:T(2,128)} %constant_dynamic-update-slice_fusion), calls=%async_computation.3 | async-start | bytes 16384 | tf_op jit(solution)/shard_map/all_to_all | solution.py:89
  106.2 57.3 %copy-start.1 = (f32[128,128]{1,0:T(8,128)S(1)}, f32[128,128]{1,0:T(8,128)}, u32[]{:S(2)}) copy-start(f32[128,128]{1,0:T(8,128)} %param.9) | copy-start | bytes 196612
  175.0 8.8 %all-to-all-start = ((f32[4,8,128]{2,1,0:T(8,128)}), f32[4,8,128]{2,1,0:T(8,128)S(1)}, u32[]{:S(2)}, u32[]{:S(2)}) async-start(f32[4,8,128]{2,1,0:T(8,128)} %reshape.79), calls=%async_computation | async-start | bytes 32768 | tf_op jit(solution)/shard_map/all_to_all | solution.py:82
  184.5 10.7 %all-to-all-start.1 = ((f32[4,8,128]{2,0,1:T(4,128)}), f32[4,8,128]{2,0,1:T(4,128)S(1)}, u32[]{:S(2)}, u32[]{:S(2)}) async-start(f32[4,8,128]{2,0,1:T(4,128)} %copy.73), calls=%async_computation.1 | async-start | bytes 32768 | tf_op jit(solution)/shard_map/all_to_all | solution.py:81
Sparse Core Ops, SparseCore 0:
  18.6 32.7 all-gather.1
